TPU v7x, 32 devices: a whole 2x2x4 slice. The times are simulated.
32 devices in a mesh: dp: 4 (over z), row: 2 (over x), col: 4 (over y, core).
Axes of the slice: x: 2, y: 2, z: 4, core: 2. Of those that a mesh axis runs over, the one named last changes fastest.
Arguments:
- grad: bfloat16 [4, 4096, 14336], P('dp', 'row', 'col'), may hold values from -6 to 6
- error: bfloat16 [4, 4096, 14336], P('dp', 'row', 'col'), may hold values from -6 to 6
- q_init: float32 [14336, 128], P('col'), may hold values from -6 to 6
Outputs:
- new_error: bfloat16 [4, 4096, 14336], P('dp', 'row', 'col')
- q_factor: float32 [14336, 128], P('col')
All inputs are finite; a program needn't handle non-finite values.
Results may differ from a plain program's by a relative error of at most 0.001.
Values sent between devices are 32-bit elements; how exact they have to be, the bound alone decides.
A program may use at most 128 MiB of HBM per device.

v0:
```python
import jax
import jax.numpy as jnp
from jax import lax
from jax.sharding import PartitionSpec as P

ITERS = 2


def solve_rows(p_mat, gram):
    lower = jnp.linalg.cholesky(gram)
    return jax.scipy.linalg.solve_triangular(lower, p_mat.T, lower=True).T


def self_gram(p_mat):
    return jnp.dot(
        p_mat.T, p_mat, precision=lax.Precision.HIGHEST, preferred_element_type=jnp.float32
    )


def shards(grad, error, q_init):
    comp = grad[0].astype(jnp.float32) + error[0].astype(jnp.float32)
    scale = 1.0 / lax.axis_size("dp")
    q_mat = q_init
    p_hat = None
    for step in range(ITERS):
        partial_value = jnp.dot(
            comp, q_mat, precision=lax.Precision.HIGHEST, preferred_element_type=jnp.float32
        )
        summed = lax.psum(lax.psum(partial_value, "col"), "dp")
        p_mat = summed * scale
        gram = lax.psum(self_gram(p_mat), "row")
        p_hat = solve_rows(p_mat, gram)
        term = lax.dot_general(
            comp,
            p_hat,
            (((0,), (0,)), ((), ())),
            precision=lax.Precision.HIGHEST,
            preferred_element_type=jnp.float32,
        )
        q_mat = lax.psum(term, ("dp", "row")) * scale
    approx = jnp.dot(
        p_hat, q_mat.T, precision=lax.Precision.HIGHEST, preferred_element_type=jnp.float32
    )
    new_error = (comp - approx).astype(jnp.bfloat16)[None]
    return (new_error, q_mat)


def solution(mesh):
    in_specs = (P("dp", "row", "col"), P("dp", "row", "col"), P("col", None))
    out_specs = (P("dp", "row", "col"), P("col", None))
    return jax.shard_map(shards, mesh=mesh, in_specs=in_specs, out_specs=out_specs, check_vma=False)
```

profile of v0, /device:TPU:0, one launch (start us, length us, event | category | flops | bytes accessed | tf_op | source)
XLA Modules:
  0.0 686.6 jit_solution(13986567056478800305)
XLA Ops:
  7.2 1.4 copy-done
  8.7 28.2 %fusion.6 = f32[2048,128]{1,0:T(8,128)} fusion(f32[3584,128]{1,0:T(8,128)S(1)} %copy-done, bf16[1,2048,3584]{2,1,0:T(8,128)(2,1)} %param.7, bf16[1,2048,3584]{2,1,0:T(8,128)(2,1)} %param.6), kind=kOutput, calls=%fused_computation.7 | convolution fusion | flops 11296309248 | bytes 32243712 | tf_op jit(solution)/shard_map/dot_general | solution.py:26
  37.0 39.1 %all-reduce.9.cloned.1.call-done = f32[2048,128]{1,0:T(8,128)} async-done(((f32[2048,128]{1,0:T(8,128)}), f32[2048,128]{1,0:T(8,128)}) %all-reduce.9.cloned.1.call-update) | async-done | bytes 1048592 | tf_op jit(solution)/shard_map/psum | solution.py:29
  76.2 54.7 %all-reduce.11.cloned.1.call-done = f32[2048,128]{1,0:T(8,128)} async-done(((f32[2048,128]{1,0:T(8,128)}), f32[2048,128]{1,0:T(8,128)}) %all-reduce.11.cloned.1.call-update) | async-done | bytes 1048592 | tf_op jit(solution)/shard_map/psum | solution.py:29
  130.9 4.0 fusion.19
  135.1 20.1 %all-reduce.13.cloned.1.call-done = f32[128,128]{0,1:T(8,128)} async-done(((f32[128,128]{0,1:T(8,128)}), f32[128,128]{0,1:T(8,128)}) %all-reduce.13.cloned.1.call-update) | async-done | bytes 65552 | tf_op jit(solution)/shard_map/psum | solution.py:31
  155.3 0.9 copy.6
  156.2 0.9 fusion.31
  157.1 11.7 %cholesky.44 = f32[128,128]{1,0:T(8,128)S(1)} custom-call(f32[128,128]{1,0:T(8,128)S(1)} %fusion.31), custom_call_target="Cholesky" | custom-call | tf_op jit(solution)/shard_map/jit(cholesky)/cholesky | solution.py:10
  168.8 0.6 compare_reduce_fusion.1
  169.4 0.7 fusion.26
  170.1 9.8 %custom-call.6 = f32[1,128,128]{1,2,0:T(8,128)S(1)} custom-call(f32[1,128,128]{2,1,0:T(8,128)S(1)} %fusion.26), custom_call_target="InvertDiagBlocksLowerTriangular" | custom-call | tf_op jit(solution)/shard_map/jit(_solve_triangular)/triangular_solve | solution.py:11
  179.9 2.3 fusion.13
  182.2 50.6 %fusion.4 = f32[3584,128]{1,0:T(8,128)} fusion(f32[128,2048]{1,0:T(8,128)S(1)} %fusion.13, bf16[1,2048,3584]{2,1,0:T(8,128)(2,1)} %param.7, bf16[1,2048,3584]{2,1,0:T(8,128)(2,1)} %param.6), kind=kOutput, calls=%fused_computation.5 | convolution fusion | flops 11296309248 | bytes 32243712 | tf_op jit(solution)/shard_map/dot_general | solution.py:33
  232.9 95.9 %all-reduce.15.cloned.1.call-done = f32[3584,128]{1,0:T(8,128)} async-done(((f32[3584,128]{1,0:T(8,128)}), f32[3584,128]{1,0:T(8,128)}) %all-reduce.15.cloned.1.call-update) | async-done | bytes 1835024 | tf_op jit(solution)/shard_map/psum | solution.py:40
  328.8 28.4 %fusion.2 = f32[2048,128]{1,0:T(8,128)} fusion(bf16[1,2048,3584]{2,1,0:T(8,128)(2,1)} %param.7, bf16[1,2048,3584]{2,1,0:T(8,128)(2,1)} %param.6, f32[3584,128]{1,0:T(8,128)} %all-reduce.15.cloned.1.call-done), kind=kOutput, calls=%fused_computation.3 | convolution fusion | flops 11296768000 | bytes 32243712 | tf_op jit(solution)/shard_map/dot_general | solution.py:26
  357.3 35.9 %all-reduce.17.cloned.1.call-done = f32[2048,128]{1,0:T(8,128)} async-done(((f32[2048,128]{1,0:T(8,128)}), f32[2048,128]{1,0:T(8,128)}) %all-reduce.17.cloned.1.call-update) | async-done | bytes 1048592 | tf_op jit(solution)/shard_map/psum | solution.py:29
  393.3 54.5 %all-reduce.19.cloned.1.call-done = f32[2048,128]{1,0:T(8,128)} async-done(((f32[2048,128]{1,0:T(8,128)}), f32[2048,128]{1,0:T(8,128)}) %all-reduce.19.cloned.1.call-update) | async-done | bytes 1048592 | tf_op jit(solution)/shard_map/psum | solution.py:29
  447.9 4.0 fusion.16
  451.9 0.5 all-reduce.23.cloned.1.call-start
  452.4 19.9 %all-reduce.21.cloned.1.call-done = f32[128,128]{0,1:T(8,128)} async-done(((f32[128,128]{0,1:T(8,128)}), f32[128,128]{0,1:T(8,128)}) %all-reduce.21.cloned.1.call-update) | async-done | bytes 65552 | tf_op jit(solution)/shard_map/psum | solution.py:31
  472.3 0.9 copy.8
  473.2 0.9 fusion.29
  474.1 11.7 %cholesky.55 = f32[128,128]{1,0:T(8,128)S(1)} custom-call(f32[128,128]{1,0:T(8,128)S(1)} %fusion.29), custom_call_target="Cholesky" | custom-call | tf_op jit(solution)/shard_map/jit(cholesky)/cholesky | solution.py:10
  485.8 0.6 compare_reduce_fusion
  486.4 0.7 fusion.27
  487.1 9.8 %custom-call.7 = f32[1,128,128]{1,2,0:T(8,128)S(1)} custom-call(f32[1,128,128]{2,1,0:T(8,128)S(1)} %fusion.27), custom_call_target="InvertDiagBlocksLowerTriangular" | custom-call | tf_op jit(solution)/shard_map/jit(_solve_triangular)/triangular_solve | solution.py:11
  496.9 2.3 fusion.11
  499.2 50.5 %fusion = f32[3584,128]{1,0:T(8,128)} fusion(f32[128,2048]{1,0:T(8,128)S(1)} %fusion.11, bf16[1,2048,3584]{2,1,0:T(8,128)(2,1)} %param.7, bf16[1,2048,3584]{2,1,0:T(8,128)(2,1)} %param.6), kind=kOutput, calls=%fused_computation.1 | convolution fusion | flops 11296309248 | bytes 32243712 | tf_op jit(solution)/shard_map/dot_general | solution.py:33
  549.7 96.0 %all-reduce.23.cloned.1.call-done = f32[3584,128]{1,0:T(8,128)} async-done(((f32[3584,128]{1,0:T(8,128)}), f32[3584,128]{1,0:T(8,128)}) %all-reduce.23.cloned.1.call-update) | async-done | bytes 1835024 | tf_op jit(solution)/shard_map/psum | solution.py:40
  645.7 1.6 broadcast_multiply_fusion
  647.3 32.2 %fusion.9 = bf16[1,2048,3584]{2,1,0:T(8,128)(2,1)} fusion(f32[128,2048]{1,0:T(8,128)S(1)} %fusion.11, f32[3584,128]{1,0:T(8,128)S(1)} %broadcast_multiply_fusion, bf16[1,2048,3584]{2,1,0:T(8,128)(2,1)} %param.7, bf16[1,2048,3584]{2,1,0:T(8,128)(2,1)} %param.6), kind=kOutput, calls=%fused_computation.11 | convolution fusion | flops 11310989312 | bytes 46923776 | tf_op jit(solution)/shard_map/dot_general | solution.py:41
  (20 shorter events, 0.7 us)
Async XLA Ops:
  7.2 1.5 copy-start
  7.2 68.9 %all-reduce.9.cloned.1.call-start = ((), (), s32[]{:S(2)}) async-start(), calls=%async_computation | async-start | bytes 2097152 | tf_op jit(solution)/shard_map/psum | solution.py:29
  36.9 93.9 %all-reduce.11.cloned.1.call-start = ((), (), s32[]{:S(2)}) async-start(), calls=%async_computation.1 | async-start | bytes 2097152 | tf_op jit(solution)/shard_map/psum | solution.py:29
  76.1 79.1 %all-reduce.13.cloned.1.call-start = ((), (), s32[]{:S(2)}) async-start(), calls=%async_computation.2 | async-start | bytes 131072 | tf_op jit(solution)/shard_map/psum | solution.py:31
  134.9 193.9 %all-reduce.15.cloned.1.call-start = ((), (), s32[]{:S(2)}) async-start(), calls=%async_computation.3 | async-start | bytes 3670016 | tf_op jit(solution)/shard_map/psum | solution.py:40
  232.9 160.4 %all-reduce.17.cloned.1.call-start = ((), (), s32[]{:S(2)}) async-start(), calls=%async_computation.4 | async-start | bytes 2097152 | tf_op jit(solution)/shard_map/psum | solution.py:29
  357.3 90.6 %all-reduce.19.cloned.1.call-start = ((), (), s32[]{:S(2)}) async-start(), calls=%async_computation.5 | async-start | bytes 2097152 | tf_op jit(solution)/shard_map/psum | solution.py:29
  393.3 79.0 %all-reduce.21.cloned.1.call-start = ((), (), s32[]{:S(2)}) async-start(), calls=%async_computation.6 | async-start | bytes 131072 | tf_op jit(solution)/shard_map/psum | solution.py:31
  451.9 193.8 %all-reduce.23.cloned.1.call-start = ((), (), s32[]{:S(2)}) async-start(), calls=%async_computation.7 | async-start | bytes 3670016 | tf_op jit(solution)/shard_map/psum | solution.py:40
  647.3 32.2 %copy-start.1 = (f32[3584,128]{1,0:T(8,128)}, f32[3584,128]{1,0:T(8,128)S(1)}, u32[]{:S(2)}) copy-start(f32[3584,128]{1,0:T(8,128)S(1)} %broadcast_multiply_fusion) | copy-start | bytes 5505028
Sparse Core Ops, SparseCore 0:
  37.1 39.0 all-reduce.8
  78.5 52.3 all-reduce.10
  135.0 20.1 all-reduce.12
  233.0 95.8 all-reduce.14
  357.4 35.8 all-reduce.16
  395.5 52.3 all-reduce.18
  452.0 20.1 all-reduce.20
  549.8 95.8 all-reduce.22
where the time goes:
time: 693 us; the launch traced here: 687 us
  waiting for transfers between devices  416 us (60%)
  matrix products  203 us (29%)
  other arithmetic  49 us (7%)
  between operations  14.5 us (2%)
    psum x2, waiting for transfers between devices, shards(): q_mat = lax.psum(term, ('dp', 'row')) * scale  192 us
    psum x4, waiting for transfers between devices, shards(): summed = lax.psum(lax.psum(partial_value, 'col'), 'dp')  184 us
    dot_general x2, matrix products, shards(): lax.dot_general(comp, p_hat, (((0,), (0,)), ((), ())), precision=lax.Prec...  101 us
    dot_general x2, matrix products, shards(): jnp.dot(comp, q_mat, precision=lax.Precision.HIGHEST, preferred_element_t...  56.7 us
    psum x2, waiting for transfers between devices, shards(): gram = lax.psum(self_gram(p_mat), 'row')  40 us
    dot_general x1, matrix products, shards(): jnp.dot(p_hat, q_mat.T, precision=lax.Precision.HIGHEST, preferred_elemen...  32.2 us
    another operation x6, other arithmetic, solve_rows(): lower = jnp.linalg.cholesky(gram)  24.8 us
    another operation x4, other arithmetic, solve_rows(): return jax.scipy.linalg.solve_triangular(lower, p_mat.T, lower=True).T  20.9 us
  transfers between devices with their start and end apart: 8, of which 8 were waited for; matrix products, arithmetic and copies ran while one was open for 0% of the time, Pallas kernels for 0%

commit v1 on v0

--- a/solution.py
+++ b/solution.py
@@ -28,7 +28,7 @@
         )
         summed = lax.psum(lax.psum(partial_value, "col"), "dp")
         p_mat = summed * scale
-        gram = lax.psum(self_gram(p_mat), "row")
+        gram = jnp.sum(lax.all_gather(self_gram(p_mat), "row"), axis=0)
         p_hat = solve_rows(p_mat, gram)
         term = lax.dot_general(
             comp,

time: 693 us -> 657 us (0.948)
  waiting for transfers between devices: 416 us -> 375 us
  blocking collectives: 0 us -> 10.5 us
    psum x2 -> x0, waiting for transfers between devices: 40 us -> none  [shards(): gram = lax.psum(self_gram(p_mat), 'row')]
    all_gather x0 -> x2, blocking collectives: none -> 10.5 us  [shards(): gram = jnp.sum(lax.all_gather(self_gram(p_mat), 'row'), axis=0)]
  transfers between devices with their start and end apart: 8 -> 6, of which waited for: 8 -> 6; matrix products, arithmetic and copies ran while one was open for 0% -> 0% of each run, Pallas kernels for 0% -> 0%
where the time goes in v1:
time: 657 us; the launch traced here: 651 us
  waiting for transfers between devices  375 us (57%)
  matrix products  202 us (31%)
  other arithmetic  47.4 us (7%)
  between operations  14.4 us (2%)
  blocking collectives  10.5 us (2%)
    psum x2, waiting for transfers between devices, shards(): q_mat = lax.psum(term, ('dp', 'row')) * scale  191 us
    psum x4, waiting for transfers between devices, shards(): summed = lax.psum(lax.psum(partial_value, 'col'), 'dp')  184 us
    dot_general x2, matrix products, shards(): lax.dot_general(comp, p_hat, (((0,), (0,)), ((), ())), precision=lax.Prec...  101 us
    dot_general x2, matrix products, shards(): jnp.dot(comp, q_mat, precision=lax.Precision.HIGHEST, preferred_element_t...  56.7 us
    dot_general x1, matrix products, shards(): jnp.dot(p_hat, q_mat.T, precision=lax.Precision.HIGHEST, preferred_elemen...  32.2 us
    another operation x6, other arithmetic, solve_rows(): lower = jnp.linalg.cholesky(gram)  24.8 us
    another operation x4, other arithmetic, solve_rows(): return jax.scipy.linalg.solve_triangular(lower, p_mat.T, lower=True).T  20.9 us
  transfers between devices with their start and end apart: 6, of which 6 were waited for; matrix products, arithmetic and copies ran while one was open for 0% of the time, Pallas kernels for 0%

profile of v1, /device:TPU:0, one launch (start us, length us, event | category | flops | bytes accessed | tf_op | source)
XLA Modules:
  0.0 650.7 jit_solution(6218776032691773403)
XLA Ops:
  7.2 1.4 copy-done
  8.7 28.2 %fusion.6 = f32[2048,128]{1,0:T(8,128)} fusion(f32[3584,128]{1,0:T(8,128)S(1)} %copy-done, bf16[1,2048,3584]{2,1,0:T(8,128)(2,1)} %param.7, bf16[1,2048,3584]{2,1,0:T(8,128)(2,1)} %param.6), kind=kOutput, calls=%fused_computation.7 | convolution fusion | flops 11296309248 | bytes 32243712 | tf_op jit(solution)/shard_map/dot_general | solution.py:26
  36.9 0.0 all-reduce.9.cloned.1.call-start
  37.0 39.1 %all-reduce.7.cloned.1.call-done = f32[2048,128]{1,0:T(8,128)} async-done(((f32[2048,128]{1,0:T(8,128)}), f32[2048,128]{1,0:T(8,128)}) %all-reduce.7.cloned.1.call-update) | async-done | bytes 1048592 | tf_op jit(solution)/shard_map/psum | solution.py:29
  76.2 54.7 %all-reduce.9.cloned.1.call-done = f32[2048,128]{1,0:T(8,128)} async-done(((f32[2048,128]{1,0:T(8,128)}), f32[2048,128]{1,0:T(8,128)}) %all-reduce.9.cloned.1.call-update) | async-done | bytes 1048592 | tf_op jit(solution)/shard_map/psum | solution.py:29
  130.8 3.5 fusion.19
  134.4 5.1 all-gather
  139.5 0.1 copy.7
  139.6 11.7 %cholesky.44 = f32[128,128]{1,0:T(8,128)S(1)} custom-call(f32[128,128]{1,0:T(8,128)S(1)} %fusion.31), custom_call_target="Cholesky" | custom-call | tf_op jit(solution)/shard_map/jit(cholesky)/cholesky | solution.py:10
  151.3 0.6 compare_reduce_fusion.1
  152.0 0.7 fusion.26
  152.6 9.8 %custom-call.6 = f32[1,128,128]{1,2,0:T(8,128)S(1)} custom-call(f32[1,128,128]{2,1,0:T(8,128)S(1)} %fusion.26), custom_call_target="InvertDiagBlocksLowerTriangular" | custom-call | tf_op jit(solution)/shard_map/jit(_solve_triangular)/triangular_solve | solution.py:11
  162.5 2.3 fusion.13
  164.8 50.6 %fusion.4 = f32[3584,128]{1,0:T(8,128)} fusion(f32[128,2048]{1,0:T(8,128)S(1)} %fusion.13, bf16[1,2048,3584]{2,1,0:T(8,128)(2,1)} %param.7, bf16[1,2048,3584]{2,1,0:T(8,128)(2,1)} %param.6), kind=kOutput, calls=%fused_computation.5 | convolution fusion | flops 11296309248 | bytes 32243712 | tf_op jit(solution)/shard_map/dot_general | solution.py:33
  215.4 0.0 all-reduce.13.cloned.1.call-start
  215.5 95.3 %all-reduce.11.cloned.1.call-done = f32[3584,128]{1,0:T(8,128)} async-done(((f32[3584,128]{1,0:T(8,128)}), f32[3584,128]{1,0:T(8,128)}) %all-reduce.11.cloned.1.call-update) | async-done | bytes 1835024 | tf_op jit(solution)/shard_map/psum | solution.py:40
  310.7 28.4 %fusion.2 = f32[2048,128]{1,0:T(8,128)} fusion(bf16[1,2048,3584]{2,1,0:T(8,128)(2,1)} %param.7, bf16[1,2048,3584]{2,1,0:T(8,128)(2,1)} %param.6, f32[3584,128]{1,0:T(8,128)} %all-reduce.11.cloned.1.call-done), kind=kOutput, calls=%fused_computation.3 | convolution fusion | flops 11296768000 | bytes 32243712 | tf_op jit(solution)/shard_map/dot_general | solution.py:26
  339.2 0.0 all-reduce.15.cloned.1.call-start
  339.2 35.9 %all-reduce.13.cloned.1.call-done = f32[2048,128]{1,0:T(8,128)} async-done(((f32[2048,128]{1,0:T(8,128)}), f32[2048,128]{1,0:T(8,128)}) %all-reduce.13.cloned.1.call-update) | async-done | bytes 1048592 | tf_op jit(solution)/shard_map/psum | solution.py:29
  375.2 54.5 %all-reduce.15.cloned.1.call-done = f32[2048,128]{1,0:T(8,128)} async-done(((f32[2048,128]{1,0:T(8,128)}), f32[2048,128]{1,0:T(8,128)}) %all-reduce.15.cloned.1.call-update) | async-done | bytes 1048592 | tf_op jit(solution)/shard_map/psum | solution.py:29
  429.7 3.5 fusion.16
  433.3 5.4 all-gather.1
  438.7 0.1 copy.8
  438.8 11.7 %cholesky.55 = f32[128,128]{1,0:T(8,128)S(1)} custom-call(f32[128,128]{1,0:T(8,128)S(1)} %fusion.29), custom_call_target="Cholesky" | custom-call | tf_op jit(solution)/shard_map/jit(cholesky)/cholesky | solution.py:10
  450.5 0.6 compare_reduce_fusion
  451.2 0.7 fusion.27
  451.8 9.8 %custom-call.7 = f32[1,128,128]{1,2,0:T(8,128)S(1)} custom-call(f32[1,128,128]{2,1,0:T(8,128)S(1)} %fusion.27), custom_call_target="InvertDiagBlocksLowerTriangular" | custom-call | tf_op jit(solution)/shard_map/jit(_solve_triangular)/triangular_solve | solution.py:11
  461.7 2.3 fusion.11
  464.0 50.5 %fusion = f32[3584,128]{1,0:T(8,128)} fusion(f32[128,2048]{1,0:T(8,128)S(1)} %fusion.11, bf16[1,2048,3584]{2,1,0:T(8,128)(2,1)} %param.7, bf16[1,2048,3584]{2,1,0:T(8,128)(2,1)} %param.6), kind=kOutput, calls=%fused_computation.1 | convolution fusion | flops 11296309248 | bytes 32243712 | tf_op jit(solution)/shard_map/dot_general | solution.py:33
  514.4 95.3 %all-reduce.17.cloned.1.call-done = f32[3584,128]{1,0:T(8,128)} async-done(((f32[3584,128]{1,0:T(8,128)}), f32[3584,128]{1,0:T(8,128)}) %all-reduce.17.cloned.1.call-update) | async-done | bytes 1835024 | tf_op jit(solution)/shard_map/psum | solution.py:40
  609.7 1.6 broadcast_multiply_fusion
  611.4 32.2 %fusion.9 = bf16[1,2048,3584]{2,1,0:T(8,128)(2,1)} fusion(f32[128,2048]{1,0:T(8,128)S(1)} %fusion.11, f32[3584,128]{1,0:T(8,128)S(1)} %broadcast_multiply_fusion, bf16[1,2048,3584]{2,1,0:T(8,128)(2,1)} %param.7, bf16[1,2048,3584]{2,1,0:T(8,128)(2,1)} %param.6), kind=kOutput, calls=%fused_computation.11 | convolution fusion | flops 11310989312 | bytes 46923776 | tf_op jit(solution)/shard_map/dot_general | solution.py:41
  (18 shorter events, 0.3 us)
Async XLA Ops:
  7.2 1.5 copy-start
  7.2 68.9 %all-reduce.7.cloned.1.call-start = ((), (), s32[]{:S(2)}) async-start(), calls=%async_computation | async-start | bytes 2097152 | tf_op jit(solution)/shard_map/psum | solution.py:29
  36.9 93.9 %all-reduce.9.cloned.1.call-start = ((), (), s32[]{:S(2)}) async-start(), calls=%async_computation.1 | async-start | bytes 2097152 | tf_op jit(solution)/shard_map/psum | solution.py:29
  76.1 234.6 %all-reduce.11.cloned.1.call-start = ((), (), s32[]{:S(2)}) async-start(), calls=%async_computation.2 | async-start | bytes 3670016 | tf_op jit(solution)/shard_map/psum | solution.py:40
  215.4 159.7 %all-reduce.13.cloned.1.call-start = ((), (), s32[]{:S(2)}) async-start(), calls=%async_computation.3 | async-start | bytes 2097152 | tf_op jit(solution)/shard_map/psum | solution.py:29
  339.2 90.6 %all-reduce.15.cloned.1.call-start = ((), (), s32[]{:S(2)}) async-start(), calls=%async_computation.4 | async-start | bytes 2097152 | tf_op jit(solution)/shard_map/psum | solution.py:29
  375.2 234.6 %all-reduce.17.cloned.1.call-start = ((), (), s32[]{:S(2)}) async-start(), calls=%async_computation.5 | async-start | bytes 3670016 | tf_op jit(solution)/shard_map/psum | solution.py:40
  611.4 32.2 %copy-start.1 = (f32[3584,128]{1,0:T(8,128)}, f32[3584,128]{1,0:T(8,128)S(1)}, u32[]{:S(2)}) copy-start(f32[3584,128]{1,0:T(8,128)S(1)} %broadcast_multiply_fusion) | copy-start | bytes 5505028
Sparse Core Ops, SparseCore 0:
  37.1 38.9 all-reduce.6
  78.4 52.3 all-reduce.8
  215.5 95.1 all-reduce.10
  339.3 35.8 all-reduce.12
  377.4 52.3 all-reduce.14
  514.6 95.1 all-reduce.16
